TPU v7x, 32 devices: a whole 2x2x4 slice. The times are simulated.
32 devices in a mesh: blk: 16 (over z, y, core), team: 2 (over x).
Axes of the slice: x: 2, y: 2, z: 4, core: 2. Of those that a mesh axis runs over, the one named last changes fastest.
Arguments:
- positions: float32 [16384, 3], P('blk'), may hold values from 0 to 1
- velocity: float32 [16384, 3], P('blk'), may hold values from -6 to 6
- masses: float32 [16384], P('blk'), may hold values from 6.1035157e-06 to 0.00061035156
Outputs:
- accel: float32 [16384, 3], P('blk')
- velocity_next: float32 [16384, 3], P('blk')
- positions_next: float32 [16384, 3], P('blk')
All inputs are finite; a program needn't handle non-finite values.
Results may differ from a plain program's by a relative error of at most 0.0003.
Values sent between devices are 32-bit elements.
A program may use at most 64 MiB of HBM per device.

v0:
```python
import jax
import jax.numpy as jnp
from jax import lax
from jax.sharding import PartitionSpec as P

SOFTEN_SQ = 0.0004
TIME_STEP = 0.01


def passed_along(block, axis, distance):
    devices = range(lax.axis_size(axis))
    route = [((i - distance) % len(devices), i) for i in devices]
    return lax.ppermute(block, axis, route)


def attract(targets, sources):
    deltas = [sources[None, :, column] - targets[:, column : column + 1] for column in range(3)]
    dist_sq = deltas[0] * deltas[0] + deltas[1] * deltas[1] + deltas[2] * deltas[2] + SOFTEN_SQ
    inverse = lax.rsqrt(dist_sq)
    weight = sources[None, :, 3] * inverse * inverse * inverse
    return jnp.stack([jnp.sum(weight * delta, axis=1) for delta in deltas], axis=1)


def per_device(positions, velocity, masses):
    packed = jnp.concatenate([positions, masses[:, None]], axis=1)
    blocks = lax.axis_size("blk")
    half = blocks // 2
    member = lax.axis_index("team")
    rows = positions.shape[0]
    following = passed_along(packed, "blk", -1)
    doubled = jnp.concatenate([packed, following], axis=0)
    far = passed_along(doubled, "blk", -half)
    carried = jnp.where(member == 1, far, doubled)

    def advance_pair(counter, state):
        summed, holding = state
        summed = summed + attract(positions, holding)
        return (summed, passed_along(holding, "blk", -2))

    summed, carried = lax.fori_loop(
        0, half // 2 - 1, advance_pair, (jnp.zeros((rows, 3), jnp.float32), carried)
    )
    summed = summed + attract(positions, carried)
    accel = lax.psum(summed, "team")
    velocity_next = velocity + TIME_STEP * accel
    positions_next = positions + TIME_STEP * velocity_next
    return (accel, velocity_next, positions_next)


def solution(mesh):
    in_specs = (P("blk", None), P("blk", None), P("blk"))
    out_specs = (P("blk", None), P("blk", None), P("blk", None))
    return jax.shard_map(
        per_device, mesh=mesh, in_specs=in_specs, out_specs=out_specs, check_vma=False
    )
```

profile of v0, /device:TPU:0, one launch (start us, length us, event | category | flops | bytes accessed | tf_op | source)
XLA Modules:
  0.0 52.1 jit_solution(14040459949676174283)
XLA Ops:
  0.6 0.0 copy-start.2
  0.6 0.0 copy-start
  0.6 0.8 %pad_maximum_fusion.1 = f32[1024,4]{0,1:T(4,128)S(1)} fusion(f32[1024,1]{0,1:T(1,128)} %bitcast.51, f32[1024,3]{0,1:T(4,128)} %param.5), kind=kLoop, calls=%fused_computation.30 | loop fusion | flops 4096 | bytes 32768 | tf_op jit(solution)/shard_map/concatenate | solution.py:25
  1.4 5.5 %collective-permute-start.1 = (f32[1024,4]{0,1:T(4,128)S(1)}, f32[1024,4]{0,1:T(4,128)S(1)}, u32[]{:S(2)}, u32[]{:S(2)}) collective-permute-start(f32[1024,4]{0,1:T(4,128)S(1)} %pad_maximum_fusion.1), channel_id=1, source_target_pairs={{2,0},{4,2},{6,4},{8,6},{10,8},{12,10},{14,12},{16,14},{18,16},{20... | collective-permute-start | bytes 49160 | tf_op jit(solution)/shard_map/ppermute | solution.py:13
  7.0 1.4 %collective-permute-done.1 = f32[1024,4]{0,1:T(4,128)S(1)} collective-permute-done((f32[1024,4]{0,1:T(4,128)S(1)}, f32[1024,4]{0,1:T(4,128)S(1)}, u32[]{:S(2)}, u32[]{:S(2)}) %collective-permute-start.1) | collective-permute-done | bytes 16416 | tf_op jit(solution)/shard_map/ppermute | solution.py:13
  8.4 0.0 copy-done.2
  8.4 0.0 copy-done
  8.4 0.1 collective-permute-start.2
  8.6 4.8 %collective-permute-done.2 = f32[2048,4]{0,1:T(4,128)S(1)} collective-permute-done((f32[2048,4]{0,1:T(4,128)S(1)}, f32[2048,4]{0,1:T(4,128)S(1)}, u32[]{:S(2)}, u32[]{:S(2)}) %collective-permute-start.2) | collective-permute-done | bytes 32800 | tf_op jit(solution)/shard_map/ppermute | solution.py:13
  13.3 23.2 %while.13 = (s32[]{:T(128)}, f32[1024,3]{0,1:T(4,128)S(1)}, f32[2048,4]{0,1:T(4,128)S(1)}, f32[1024,3]{0,1:T(4,128)S(1)}, s32[]{:T(128)}, /*index=5*/s32[]{:T(128)}) while((s32[]{:T(128)}, f32[1024,3]{0,1:T(4,128)S(1)}, f32[2048,4]{0,1:T(4,128)S(1)}, f32[1024,3]{0,1:T(4,128)S(1)}, s32[]{:T(128)}, /*index=5*/s32[]{:T(128)}) %tuple.50), condition=%wide.region_4.5_spmd.clone, body=%wide.region_0.4_spmd.clone.sunk | while | flops 37757952 | bytes 381047 | solution.py:40
  13.4 0.9 %collective-permute-start = (f32[2048,4]{0,1:T(4,128)S(1)}, f32[2048,4]{0,1:T(4,128)S(1)}, u32[]{:S(2)}, u32[]{:S(2)}) collective-permute-start(f32[2048,4]{0,1:T(4,128)S(1)} %copy.11), channel_id=1, source_target_pairs={{4,0},{6,2},{8,4},{10,6},{12,8},{14,10},{16,12},{18,14},{20,16},{2... | collective-permute-start | bytes 98312 | tf_op jit(solution)/shard_map/while/body/eval_jaxpr/ppermute | solution.py:13
  14.3 6.7 %fusion.23 = (f32[1024]{0:T(1024)S(1)}, f32[1024]{0:T(1024)S(1)}, f32[1024]{0:T(1024)S(1)}) fusion(f32[1024]{0:T(1024)S(1)} %bitcast.50, f32[2048]{0:T(1024)S(1)} %bitcast.44, f32[1024]{0:T(1024)S(1)} %bitcast.49, f32[2048]{0:T(1024)S(1)} %bitcast.42, f32[1024]{0:T(1024)S(1)} %bitcast.48, f32[2048]{0:T(1024)S(1)} %bitcast.43, f32[2048]{0:T(1024)S(1)} %bitcast.41), kind=kLoop, calls=%fused_computation.11.clone.1 | loop fusion | flops 37745664 | bytes 57344 | tf_op jit(solution)/shard_map/while/body/eval_jaxpr/reduce_sum | solution.py:21
  21.0 0.0 collective-permute-done
  21.0 1.9 %collective-permute-start = (f32[2048,4]{0,1:T(4,128)S(1)}, f32[2048,4]{0,1:T(4,128)S(1)}, u32[]{:S(2)}, u32[]{:S(2)}) collective-permute-start(f32[2048,4]{0,1:T(4,128)S(1)} %copy.11), channel_id=1, source_target_pairs={{4,0},{6,2},{8,4},{10,6},{12,8},{14,10},{16,12},{18,14},{20,16},{2... | collective-permute-start | bytes 98312 | tf_op jit(solution)/shard_map/while/body/eval_jaxpr/ppermute | solution.py:13
  22.9 6.7 %fusion.23 = (f32[1024]{0:T(1024)S(1)}, f32[1024]{0:T(1024)S(1)}, f32[1024]{0:T(1024)S(1)}) fusion(f32[1024]{0:T(1024)S(1)} %bitcast.50, f32[2048]{0:T(1024)S(1)} %bitcast.44, f32[1024]{0:T(1024)S(1)} %bitcast.49, f32[2048]{0:T(1024)S(1)} %bitcast.42, f32[1024]{0:T(1024)S(1)} %bitcast.48, f32[2048]{0:T(1024)S(1)} %bitcast.43, f32[2048]{0:T(1024)S(1)} %bitcast.41), kind=kLoop, calls=%fused_computation.11.clone.1 | loop fusion | flops 37745664 | bytes 57344 | tf_op jit(solution)/shard_map/while/body/eval_jaxpr/reduce_sum | solution.py:21
  29.6 0.0 collective-permute-done
  29.7 0.1 collective-permute-start
  29.8 6.7 %fusion.23 = (f32[1024]{0:T(1024)S(1)}, f32[1024]{0:T(1024)S(1)}, f32[1024]{0:T(1024)S(1)}) fusion(f32[1024]{0:T(1024)S(1)} %bitcast.50, f32[2048]{0:T(1024)S(1)} %bitcast.44, f32[1024]{0:T(1024)S(1)} %bitcast.49, f32[2048]{0:T(1024)S(1)} %bitcast.42, f32[1024]{0:T(1024)S(1)} %bitcast.48, f32[2048]{0:T(1024)S(1)} %bitcast.43, f32[2048]{0:T(1024)S(1)} %bitcast.41), kind=kLoop, calls=%fused_computation.11.clone.1 | loop fusion | flops 37745664 | bytes 57344 | tf_op jit(solution)/shard_map/while/body/eval_jaxpr/reduce_sum | solution.py:21
  36.5 0.0 collective-permute-done
  36.6 6.7 %fusion.11 = (f32[1024]{0:T(1024)S(1)}, f32[1024]{0:T(1024)S(1)}, f32[1024]{0:T(1024)S(1)}) fusion(f32[1024]{0:T(1024)S(1)} %bitcast.59, f32[2048]{0:T(1024)S(1)} %bitcast.55, f32[1024]{0:T(1024)S(1)} %bitcast.60, f32[2048]{0:T(1024)S(1)} %bitcast.56, f32[1024]{0:T(1024)S(1)} %bitcast.58, f32[2048]{0:T(1024)S(1)} %bitcast.57, f32[2048]{0:T(1024)S(1)} %bitcast.54), kind=kLoop, calls=%fused_computation.26 | loop fusion | flops 37745664 | bytes 57344 | tf_op jit(solution)/shard_map/reduce_sum | solution.py:21
  43.2 0.0 copy-start.3
  43.3 8.1 %psum.7 = f32[1024,3]{0,1:T(4,128)S(1)} all-reduce(f32[1024,3]{0,1:T(4,128)S(1)} %maximum_add_fusion.1), channel_id=1, replica_groups=mesh['blk'=16,'team'=2] {'team'}, use_global_device_ids=true, to_apply=%region_8.9 | all-reduce | flops 3072 | bytes 24576 | tf_op jit(solution)/shard_map/psum | solution.py:44
  51.4 0.0 copy-done.3
  51.4 0.6 %multiply_add_fusion = (f32[1024,3]{0,1:T(4,128)}, f32[1024,3]{0,1:T(4,128)}) fusion(f32[1024,3]{0,1:T(4,128)S(1)} %get-tuple-element.138, f32[1024,3]{0,1:T(4,128)S(1)} %copy-done.3, f32[1024,3]{0,1:T(4,128)S(1)} %psum.7), kind=kLoop, calls=%fused_computation.32 | loop fusion | flops 12288 | bytes 61440 | tf_op jit(solution)/shard_map/add | solution.py:46
  (20 shorter events, 0.3 us)
Async XLA Ops:
  0.6 7.8 %copy-start.2 = (f32[1024]{0:T(1024)S(1)}, f32[1024]{0:T(1024)}, u32[]{:S(2)}) copy-start(f32[1024]{0:T(1024)} %param.7) | copy-start | bytes 12292
  0.6 7.8 %copy-start = (f32[1024,3]{0,1:T(4,128)S(1)}, f32[1024,3]{0,1:T(4,128)}, u32[]{:S(2)}) copy-start(f32[1024,3]{0,1:T(4,128)} %param.5) | copy-start | bytes 36868
  1.4 7.0 %collective-permute-start.1 = (f32[1024,4]{0,1:T(4,128)S(1)}, f32[1024,4]{0,1:T(4,128)S(1)}, u32[]{:S(2)}, u32[]{:S(2)}) collective-permute-start(f32[1024,4]{0,1:T(4,128)S(1)} %pad_maximum_fusion.1), channel_id=1, source_target_pairs={{2,0},{4,2},{6,4},{8,6},{10,8},{12,10},{14,12},{16,14},{18,16},{20... | collective-permute-start | bytes 49160 | tf_op jit(solution)/shard_map/ppermute | solution.py:13
  8.4 4.9 %collective-permute-start.2 = (f32[2048,4]{0,1:T(4,128)S(1)}, f32[2048,4]{0,1:T(4,128)S(1)}, u32[]{:S(2)}, u32[]{:S(2)}) collective-permute-start(f32[2048,4]{0,1:T(4,128)S(1)} %pad_maximum_fusion), channel_id=1, source_target_pairs={{16,0},{18,2},{20,4},{22,6},{24,8},{26,10},{28,12},{30,14},{0,16},... | collective-permute-start | bytes 98312 | tf_op jit(solution)/shard_map/ppermute | solution.py:13
  13.4 7.6 %collective-permute-start = (f32[2048,4]{0,1:T(4,128)S(1)}, f32[2048,4]{0,1:T(4,128)S(1)}, u32[]{:S(2)}, u32[]{:S(2)}) collective-permute-start(f32[2048,4]{0,1:T(4,128)S(1)} %copy.11), channel_id=1, source_target_pairs={{4,0},{6,2},{8,4},{10,6},{12,8},{14,10},{16,12},{18,14},{20,16},{2... | collective-permute-start | bytes 98312 | tf_op jit(solution)/shard_map/while/body/eval_jaxpr/ppermute | solution.py:13
  21.0 8.6 %collective-permute-start = (f32[2048,4]{0,1:T(4,128)S(1)}, f32[2048,4]{0,1:T(4,128)S(1)}, u32[]{:S(2)}, u32[]{:S(2)}) collective-permute-start(f32[2048,4]{0,1:T(4,128)S(1)} %copy.11), channel_id=1, source_target_pairs={{4,0},{6,2},{8,4},{10,6},{12,8},{14,10},{16,12},{18,14},{20,16},{2... | collective-permute-start | bytes 98312 | tf_op jit(solution)/shard_map/while/body/eval_jaxpr/ppermute | solution.py:13
  29.7 6.9 %collective-permute-start = (f32[2048,4]{0,1:T(4,128)S(1)}, f32[2048,4]{0,1:T(4,128)S(1)}, u32[]{:S(2)}, u32[]{:S(2)}) collective-permute-start(f32[2048,4]{0,1:T(4,128)S(1)} %copy.11), channel_id=1, source_target_pairs={{4,0},{6,2},{8,4},{10,6},{12,8},{14,10},{16,12},{18,14},{20,16},{2... | collective-permute-start | bytes 98312 | tf_op jit(solution)/shard_map/while/body/eval_jaxpr/ppermute | solution.py:13
  43.2 8.2 %copy-start.3 = (f32[1024,3]{0,1:T(4,128)S(1)}, f32[1024,3]{0,1:T(4,128)}, u32[]{:S(2)}) copy-start(f32[1024,3]{0,1:T(4,128)} %param.6) | copy-start | bytes 36868
  51.4 0.6 %copy-start.1 = (f32[1024,3]{0,1:T(4,128)}, f32[1024,3]{0,1:T(4,128)S(1)}, u32[]{:S(2)}) copy-start(f32[1024,3]{0,1:T(4,128)S(1)} %psum.7) | copy-start | bytes 36868
where the time goes:
time: 52.3 us; the launch traced here: 52.1 us
  other arithmetic  28.2 us (54%)
  starting transfers between devices  8.48 us (16%)
  blocking collectives  8.15 us (16%)
  waiting for transfers between devices  6.22 us (12%)
  between operations  0.73 us (1%)
    reduce_sum x4, other arithmetic, attract(): jnp.sum(weight * delta, axis=1)  26.6 us
    ppermute x5, starting transfers between devices, passed_along(): return lax.ppermute(block, axis, route)  8.48 us
    psum x1, blocking collectives, per_device(): accel = lax.psum(summed, 'team')  8.15 us
    ppermute x5, waiting for transfers between devices, passed_along(): return lax.ppermute(block, axis, route)  6.22 us
  transfers between devices with their start and end apart: 5, of which 2 were waited for; matrix products, arithmetic and copies ran while one was open for 39% of the time, Pallas kernels for 0%

commit v1 on v0

--- a/solution.py
+++ b/solution.py
@@ -41,7 +41,7 @@
         0, half // 2 - 1, advance_pair, (jnp.zeros((rows, 3), jnp.float32), carried)
     )
     summed = summed + attract(positions, carried)
-    accel = lax.psum(summed, "team")
+    accel = jnp.sum(lax.all_gather(summed, "team"), axis=0)
     velocity_next = velocity + TIME_STEP * accel
     positions_next = positions + TIME_STEP * velocity_next
     return (accel, velocity_next, positions_next)

time: 52.3 us -> 49.4 us (0.945)
  blocking collectives: 8.15 us -> 4.41 us
  local copies, waits for them, and re-layouts: 0.17 us -> 0.87 us
    psum x1 -> x0, blocking collectives: 8.15 us -> none  [per_device(): accel = lax.psum(summed, 'team')]
    all_gather x0 -> x1, blocking collectives: none -> 4.41 us  [per_device(): accel = jnp.sum(lax.all_gather(summed, 'team'), axis=0)]
    unnamed x8, local copies, waits for them, and re-layouts: 0.02 us -> 0.68 us
  transfers between devices with their start and end apart: 5 -> 5, of which waited for: 2 -> 2; matrix products, arithmetic and copies ran while one was open for 39% -> 41% of each run, Pallas kernels for 0% -> 0%
where the time goes in v1:
time: 49.4 us; the launch traced here: 49.1 us
  other arithmetic  28.2 us (57%)
  starting transfers between devices  8.48 us (17%)
  waiting for transfers between devices  6.22 us (13%)
  blocking collectives  4.41 us (9%)
  local copies, waits for them, and re-layouts  0.87 us (2%)
  between operations  0.73 us (1%)
    reduce_sum x4, other arithmetic, attract(): jnp.sum(weight * delta, axis=1)  26.6 us
    ppermute x5, starting transfers between devices, passed_along(): return lax.ppermute(block, axis, route)  8.48 us
    ppermute x5, waiting for transfers between devices, passed_along(): return lax.ppermute(block, axis, route)  6.22 us
    all_gather x1, blocking collectives, per_device(): accel = jnp.sum(lax.all_gather(summed, 'team'), axis=0)  4.41 us
  transfers between devices with their start and end apart: 5, of which 2 were waited for; matrix products, arithmetic and copies ran while one was open for 41% of the time, Pallas kernels for 0%

profile of v1, /device:TPU:0, one launch (start us, length us, event | category | flops | bytes accessed | tf_op | source)
XLA Modules:
  0.0 49.1 jit_solution(1359402330956037544)
XLA Ops:
  0.6 0.0 copy-start.2
  0.6 0.0 copy-start
  0.6 0.8 %pad_maximum_fusion.1 = f32[1024,4]{0,1:T(4,128)S(1)} fusion(f32[1024,1]{0,1:T(1,128)} %bitcast.53, f32[1024,3]{0,1:T(4,128)} %param.5), kind=kLoop, calls=%fused_computation.30 | loop fusion | flops 4096 | bytes 32768 | tf_op jit(solution)/shard_map/concatenate | solution.py:25
  1.4 5.5 %collective-permute-start.1 = (f32[1024,4]{0,1:T(4,128)S(1)}, f32[1024,4]{0,1:T(4,128)S(1)}, u32[]{:S(2)}, u32[]{:S(2)}) collective-permute-start(f32[1024,4]{0,1:T(4,128)S(1)} %pad_maximum_fusion.1), channel_id=1, source_target_pairs={{2,0},{4,2},{6,4},{8,6},{10,8},{12,10},{14,12},{16,14},{18,16},{20... | collective-permute-start | bytes 49160 | tf_op jit(solution)/shard_map/ppermute | solution.py:13
  7.0 1.4 %collective-permute-done.1 = f32[1024,4]{0,1:T(4,128)S(1)} collective-permute-done((f32[1024,4]{0,1:T(4,128)S(1)}, f32[1024,4]{0,1:T(4,128)S(1)}, u32[]{:S(2)}, u32[]{:S(2)}) %collective-permute-start.1) | collective-permute-done | bytes 16416 | tf_op jit(solution)/shard_map/ppermute | solution.py:13
  8.4 0.0 copy-done.2
  8.4 0.0 copy-done
  8.4 0.1 collective-permute-start.2
  8.6 4.8 %collective-permute-done.2 = f32[2048,4]{0,1:T(4,128)S(1)} collective-permute-done((f32[2048,4]{0,1:T(4,128)S(1)}, f32[2048,4]{0,1:T(4,128)S(1)}, u32[]{:S(2)}, u32[]{:S(2)}) %collective-permute-start.2) | collective-permute-done | bytes 32800 | tf_op jit(solution)/shard_map/ppermute | solution.py:13
  13.3 23.2 %while.13 = (s32[]{:T(128)}, f32[1024,3]{0,1:T(4,128)S(1)}, f32[2048,4]{0,1:T(4,128)S(1)}, f32[1024,3]{0,1:T(4,128)S(1)}, s32[]{:T(128)}, /*index=5*/s32[]{:T(128)}) while((s32[]{:T(128)}, f32[1024,3]{0,1:T(4,128)S(1)}, f32[2048,4]{0,1:T(4,128)S(1)}, f32[1024,3]{0,1:T(4,128)S(1)}, s32[]{:T(128)}, /*index=5*/s32[]{:T(128)}) %tuple.50), condition=%wide.region_4.5_spmd.clone, body=%wide.region_0.4_spmd.clone.sunk | while | flops 37757952 | bytes 381047 | solution.py:40
  13.4 0.9 %collective-permute-start = (f32[2048,4]{0,1:T(4,128)S(1)}, f32[2048,4]{0,1:T(4,128)S(1)}, u32[]{:S(2)}, u32[]{:S(2)}) collective-permute-start(f32[2048,4]{0,1:T(4,128)S(1)} %copy.11), channel_id=1, source_target_pairs={{4,0},{6,2},{8,4},{10,6},{12,8},{14,10},{16,12},{18,14},{20,16},{2... | collective-permute-start | bytes 98312 | tf_op jit(solution)/shard_map/while/body/eval_jaxpr/ppermute | solution.py:13
  14.3 6.7 %fusion.23 = (f32[1024]{0:T(1024)S(1)}, f32[1024]{0:T(1024)S(1)}, f32[1024]{0:T(1024)S(1)}) fusion(f32[1024]{0:T(1024)S(1)} %bitcast.52, f32[2048]{0:T(1024)S(1)} %bitcast.46, f32[1024]{0:T(1024)S(1)} %bitcast.51, f32[2048]{0:T(1024)S(1)} %bitcast.44, f32[1024]{0:T(1024)S(1)} %bitcast.50, f32[2048]{0:T(1024)S(1)} %bitcast.45, f32[2048]{0:T(1024)S(1)} %bitcast.43), kind=kLoop, calls=%fused_computation.11.clone.1 | loop fusion | flops 37745664 | bytes 57344 | tf_op jit(solution)/shard_map/while/body/eval_jaxpr/reduce_sum | solution.py:21
  21.0 0.0 collective-permute-done
  21.0 1.9 %collective-permute-start = (f32[2048,4]{0,1:T(4,128)S(1)}, f32[2048,4]{0,1:T(4,128)S(1)}, u32[]{:S(2)}, u32[]{:S(2)}) collective-permute-start(f32[2048,4]{0,1:T(4,128)S(1)} %copy.11), channel_id=1, source_target_pairs={{4,0},{6,2},{8,4},{10,6},{12,8},{14,10},{16,12},{18,14},{20,16},{2... | collective-permute-start | bytes 98312 | tf_op jit(solution)/shard_map/while/body/eval_jaxpr/ppermute | solution.py:13
  22.9 6.7 %fusion.23 = (f32[1024]{0:T(1024)S(1)}, f32[1024]{0:T(1024)S(1)}, f32[1024]{0:T(1024)S(1)}) fusion(f32[1024]{0:T(1024)S(1)} %bitcast.52, f32[2048]{0:T(1024)S(1)} %bitcast.46, f32[1024]{0:T(1024)S(1)} %bitcast.51, f32[2048]{0:T(1024)S(1)} %bitcast.44, f32[1024]{0:T(1024)S(1)} %bitcast.50, f32[2048]{0:T(1024)S(1)} %bitcast.45, f32[2048]{0:T(1024)S(1)} %bitcast.43), kind=kLoop, calls=%fused_computation.11.clone.1 | loop fusion | flops 37745664 | bytes 57344 | tf_op jit(solution)/shard_map/while/body/eval_jaxpr/reduce_sum | solution.py:21
  29.6 0.0 collective-permute-done
  29.7 0.1 collective-permute-start
  29.8 6.7 %fusion.23 = (f32[1024]{0:T(1024)S(1)}, f32[1024]{0:T(1024)S(1)}, f32[1024]{0:T(1024)S(1)}) fusion(f32[1024]{0:T(1024)S(1)} %bitcast.52, f32[2048]{0:T(1024)S(1)} %bitcast.46, f32[1024]{0:T(1024)S(1)} %bitcast.51, f32[2048]{0:T(1024)S(1)} %bitcast.44, f32[1024]{0:T(1024)S(1)} %bitcast.50, f32[2048]{0:T(1024)S(1)} %bitcast.45, f32[2048]{0:T(1024)S(1)} %bitcast.43), kind=kLoop, calls=%fused_computation.11.clone.1 | loop fusion | flops 37745664 | bytes 57344 | tf_op jit(solution)/shard_map/while/body/eval_jaxpr/reduce_sum | solution.py:21
  36.5 0.0 collective-permute-done
  36.6 6.7 %fusion.11 = (f32[1024]{0:T(1024)S(1)}, f32[1024]{0:T(1024)S(1)}, f32[1024]{0:T(1024)S(1)}) fusion(f32[1024]{0:T(1024)S(1)} %bitcast.61, f32[2048]{0:T(1024)S(1)} %bitcast.57, f32[1024]{0:T(1024)S(1)} %bitcast.62, f32[2048]{0:T(1024)S(1)} %bitcast.58, f32[1024]{0:T(1024)S(1)} %bitcast.60, f32[2048]{0:T(1024)S(1)} %bitcast.59, f32[2048]{0:T(1024)S(1)} %bitcast.56), kind=kLoop, calls=%fused_computation.26 | loop fusion | flops 37745664 | bytes 57344 | tf_op jit(solution)/shard_map/reduce_sum | solution.py:21
  43.3 4.4 %all-gather = f32[2048,3]{0,1:T(4,128)S(1)} all-gather(f32[1024,3]{0,1:T(4,128)S(1)} %maximum_add_fusion.1), channel_id=2, replica_groups=mesh['blk'=16,'team'=2] {'team'}, dimensions={0}, use_global_device_ids=true | all-gather | bytes 36864 | tf_op jit(solution)/shard_map/all_gather | solution.py:44
  47.7 0.0 copy-start.3
  47.8 0.7 %copy-done.3 = f32[1024,3]{0,1:T(4,128)S(1)} copy-done((f32[1024,3]{0,1:T(4,128)S(1)}, f32[1024,3]{0,1:T(4,128)}, u32[]{:S(2)}) %copy-start.3) | copy-done | bytes 12312
  48.4 0.6 %multiply_add_fusion = (f32[1024,3]{0,1:T(4,128)}, f32[1024,3]{0,1:T(4,128)}) fusion(f32[1024,3]{0,1:T(4,128)S(1)} %get-tuple-element.138, f32[1024,3]{0,1:T(4,128)S(1)} %copy-done.3, f32[1024,3]{0,1:T(4,128)S(1)} %reduce_sum.66), kind=kLoop, calls=%fused_computation.32 | loop fusion | flops 12288 | bytes 61440 | tf_op jit(solution)/shard_map/add | solution.py:46
  (22 shorter events, 0.4 us)
Async XLA Ops:
  0.6 7.8 %copy-start.2 = (f32[1024]{0:T(1024)S(1)}, f32[1024]{0:T(1024)}, u32[]{:S(2)}) copy-start(f32[1024]{0:T(1024)} %param.7) | copy-start | bytes 12292
  0.6 7.8 %copy-start = (f32[1024,3]{0,1:T(4,128)S(1)}, f32[1024,3]{0,1:T(4,128)}, u32[]{:S(2)}) copy-start(f32[1024,3]{0,1:T(4,128)} %param.5) | copy-start | bytes 36868
  1.4 7.0 %collective-permute-start.1 = (f32[1024,4]{0,1:T(4,128)S(1)}, f32[1024,4]{0,1:T(4,128)S(1)}, u32[]{:S(2)}, u32[]{:S(2)}) collective-permute-start(f32[1024,4]{0,1:T(4,128)S(1)} %pad_maximum_fusion.1), channel_id=1, source_target_pairs={{2,0},{4,2},{6,4},{8,6},{10,8},{12,10},{14,12},{16,14},{18,16},{20... | collective-permute-start | bytes 49160 | tf_op jit(solution)/shard_map/ppermute | solution.py:13
  8.4 4.9 %collective-permute-start.2 = (f32[2048,4]{0,1:T(4,128)S(1)}, f32[2048,4]{0,1:T(4,128)S(1)}, u32[]{:S(2)}, u32[]{:S(2)}) collective-permute-start(f32[2048,4]{0,1:T(4,128)S(1)} %pad_maximum_fusion), channel_id=1, source_target_pairs={{16,0},{18,2},{20,4},{22,6},{24,8},{26,10},{28,12},{30,14},{0,16},... | collective-permute-start | bytes 98312 | tf_op jit(solution)/shard_map/ppermute | solution.py:13
  13.4 7.6 %collective-permute-start = (f32[2048,4]{0,1:T(4,128)S(1)}, f32[2048,4]{0,1:T(4,128)S(1)}, u32[]{:S(2)}, u32[]{:S(2)}) collective-permute-start(f32[2048,4]{0,1:T(4,128)S(1)} %copy.11), channel_id=1, source_target_pairs={{4,0},{6,2},{8,4},{10,6},{12,8},{14,10},{16,12},{18,14},{20,16},{2... | collective-permute-start | bytes 98312 | tf_op jit(solution)/shard_map/while/body/eval_jaxpr/ppermute | solution.py:13
  21.0 8.6 %collective-permute-start = (f32[2048,4]{0,1:T(4,128)S(1)}, f32[2048,4]{0,1:T(4,128)S(1)}, u32[]{:S(2)}, u32[]{:S(2)}) collective-permute-start(f32[2048,4]{0,1:T(4,128)S(1)} %copy.11), channel_id=1, source_target_pairs={{4,0},{6,2},{8,4},{10,6},{12,8},{14,10},{16,12},{18,14},{20,16},{2... | collective-permute-start | bytes 98312 | tf_op jit(solution)/shard_map/while/body/eval_jaxpr/ppermute | solution.py:13
  29.7 6.9 %collective-permute-start = (f32[2048,4]{0,1:T(4,128)S(1)}, f32[2048,4]{0,1:T(4,128)S(1)}, u32[]{:S(2)}, u32[]{:S(2)}) collective-permute-start(f32[2048,4]{0,1:T(4,128)S(1)} %copy.11), channel_id=1, source_target_pairs={{4,0},{6,2},{8,4},{10,6},{12,8},{14,10},{16,12},{18,14},{20,16},{2... | collective-permute-start | bytes 98312 | tf_op jit(solution)/shard_map/while/body/eval_jaxpr/ppermute | solution.py:13
  47.7 0.7 %copy-start.3 = (f32[1024,3]{0,1:T(4,128)S(1)}, f32[1024,3]{0,1:T(4,128)}, u32[]{:S(2)}) copy-start(f32[1024,3]{0,1:T(4,128)} %param.6) | copy-start | bytes 36868
  48.4 0.6 %copy-start.1 = (f32[1024,3]{0,1:T(4,128)}, f32[1024,3]{0,1:T(4,128)S(1)}, u32[]{:S(2)}) copy-start(f32[1024,3]{0,1:T(4,128)S(1)} %reduce_sum.66) | copy-start | bytes 36868
